TPU v7x, 128 devices: a whole 4x4x4 slice. The times are simulated.
128 devices in a mesh: row: 8 (over y, core), col: 16 (over x, z).
Axes of the slice: x: 4, y: 4, z: 4, core: 2. Of those that a mesh axis runs over, the one named last changes fastest.
Arguments:
- coupling_left: bfloat16 [128, 1024, 2048], P(('row', 'col')), may hold values from -0.75 to 0.75
- inner_factor: bfloat16 [128, 2048, 2048], P(('row', 'col')), as said below
- coupling_right: bfloat16 [128, 2048, 1024], P(('row', 'col')), may hold values from -0.75 to 0.75
- iface_rows: int32 [128, 1024], replicated, may hold values from 0 to 16383, as said below
- interface_diag: float32 [16384], P('row'), may hold values from 2 to 4
- row_scales: float32 [2, 16384], P(None, 'row'), may hold values from 0.5 to 2
- col_scales: float32 [2, 16384], P(None, 'col'), may hold values from 0.5 to 2
Outputs:
- transformed: float32 [16384, 16384], P('row', 'col')
Inputs may be any that keep to these rules, and one draw needn't show every extreme that they name: `iface_rows`: each subdomain's list is 8 runs of 128 consecutive rows, each run starting at a multiple of 128, in any order; every tile of 2048 rows holds exactly one run of every subdomain, and no tile of 1024 rows holds two runs of one subdomain. `inner_factor`: lower triangular; its diagonal lies between 0.7 and 1.3.
All inputs are finite; a program needn't handle non-finite values.
Results may differ from a plain program's by a relative error of at most 0.0003.
The roundings to bfloat16 on the way count: a program that leaves them out, or rounds other values in their place, can miss the bound.
Values sent between devices are 32-bit elements; how exact they have to be, the bound alone decides.
A program may use at most 128 MiB of HBM per device.

v0:
```python
import jax
import jax.numpy as jnp
from jax import lax
from jax.sharding import PartitionSpec as P

BROWS = 128


half_root = 0.5**0.5


def in_blocks(shard, dim, length):
    lengths = shard.shape
    parts = shard.reshape(*lengths[:dim], length, lengths[dim] // length, *lengths[dim + 1 :])
    return jnp.moveaxis(parts, dim, 0)


def joined_along(parts, dim):
    lengths = list(parts.shape[1:])
    lengths[dim] *= parts.shape[0]
    return jnp.moveaxis(parts, 0, dim).reshape(lengths)


def exchange_both(shard, axis, axes, splits, concats):
    sizes = [lax.axis_size(a) for a in axes]
    parts = in_blocks(shard, splits[0], sizes[0])
    parts = jnp.moveaxis(in_blocks(parts, splits[1] + 1, sizes[1]), 0, 1)
    inside = parts.shape[2:]
    parts = parts.reshape(-1, *inside)
    parts = lax.all_to_all(parts, axis, split_axis=0, concat_axis=0, tiled=True)
    parts = joined_along(parts.reshape(*sizes, *inside), concats[0] + 1)
    return joined_along(parts, concats[1])


def copy_for_each(shard, axis):
    length = lax.axis_size(axis)
    return lax.all_to_all(
        jnp.broadcast_to(shard[None], (length, *shard.shape)), axis, 0, 0, tiled=True
    )


def gathered_copies(shard, axis, dim):
    return joined_along(copy_for_each(shard, axis), dim)


def mix_tile_rows(spread, scales, half_tiles):
    count, strip_rows, ncols, strip_cols = spread.shape
    groups = count // (2 * half_tiles)
    shaped = spread.reshape(groups, 2, half_tiles, strip_rows, ncols, strip_cols)
    scaled = scales.reshape(groups, 2, half_tiles, strip_rows, 1, 1)
    upper = shaped[:, 0]
    lower = shaped[:, 1]
    mixed = jnp.stack([(upper + lower) * scaled[:, 0], (upper - lower) * scaled[:, 1]], axis=1)
    return (mixed * half_root).reshape(count, strip_rows, ncols, strip_cols)


def mix_tile_cols(spread, scales, half_tiles):
    nrows, strip_rows, count, strip_cols = spread.shape
    groups = count // (2 * half_tiles)
    shaped = spread.reshape(nrows, strip_rows, groups, 2, half_tiles, strip_cols)
    scaled = scales.reshape(1, 1, groups, 2, half_tiles, strip_cols)
    upper = shaped[:, :, :, 0]
    lower = shaped[:, :, :, 1]
    mixed = jnp.stack(
        [(upper + lower) * scaled[:, :, :, 0], (upper - lower) * scaled[:, :, :, 1]], axis=3
    )
    return (mixed * half_root).reshape(nrows, strip_rows, count, strip_cols)


def body(
    coupling_left, inner_factor, coupling_right, iface_rows, interface_diag, row_scales, col_scales
):
    highest = lax.Precision.HIGHEST
    row_count = lax.axis_size("row")
    col_count = lax.axis_size("col")
    device_count = row_count * col_count
    row_index = lax.axis_index("row")
    col_index = lax.axis_index("col")
    myself = row_index * col_count + col_index
    tile_rows = row_scales.shape[1]
    tile_cols = col_scales.shape[1]
    sub_count, sub_rows = iface_rows.shape
    blk_count = sub_rows // BROWS
    slot_count = blk_count // row_count
    row_blocks = tile_rows // BROWS
    col_blocks = tile_cols // BROWS
    square = BROWS * BROWS
    left_part = lax.dot_general(
        coupling_left[0],
        inner_factor[0],
        (((1,), (1,)), ((), ())),
        preferred_element_type=jnp.float32,
    ).astype(jnp.bfloat16)
    right_part = jnp.dot(
        inner_factor[0], coupling_right[0], preferred_element_type=jnp.float32
    ).astype(jnp.bfloat16)
    contribution = jnp.dot(left_part, right_part, preferred_element_type=jnp.float32)
    block_ids = iface_rows[:, ::BROWS] // BROWS
    all_rowtile = block_ids * BROWS // tile_rows
    all_coltile = block_ids * BROWS // tile_cols
    earlier = jnp.arange(blk_count)[:, None] < jnp.arange(blk_count)[None, :]
    same_tile = all_rowtile[:, :, None] == all_rowtile[:, None, :]
    all_rank = jnp.sum((same_tile & earlier[None]).astype(jnp.int32), axis=1)
    own_rowtile = lax.dynamic_slice_in_dim(all_rowtile, myself, 1, 0)[0]
    own_coltile = lax.dynamic_slice_in_dim(all_coltile, myself, 1, 0)[0]
    own_rank = lax.dynamic_slice_in_dim(all_rank, myself, 1, 0)[0]
    target = (
        (own_rowtile[:, None] * col_count + own_coltile[None, :]) * slot_count + own_rank[:, None]
    ).reshape(-1)
    selector = (jnp.arange(device_count * slot_count)[:, None] == target[None, :]).astype(
        jnp.float32
    )
    blocks = (
        contribution.reshape(blk_count, BROWS, blk_count, BROWS)
        .transpose(0, 2, 1, 3)
        .reshape(blk_count * blk_count, square)
    )
    outgoing = jnp.dot(selector, blocks, precision=highest).reshape(
        device_count, slot_count, square
    )
    incoming = lax.all_to_all(outgoing, ("row", "col"), split_axis=0, concat_axis=0, tiled=True)
    position = (block_ids[:, :, None] - row_index * row_blocks) * col_blocks + (
        block_ids[:, None, :] - col_index * col_blocks
    )
    usable = (all_rowtile[:, :, None] == row_index) & (all_coltile[:, None, :] == col_index)
    hits = (jnp.arange(row_blocks * col_blocks)[:, None, None, None] == position[None]) & usable[
        None
    ]
    hit_counts = jnp.sum(hits.astype(jnp.float32), axis=3).reshape(
        row_blocks * col_blocks, sub_count * blk_count
    )
    column_ids = (jnp.arange(sub_count)[:, None] * slot_count + all_rank).reshape(-1)
    column_pick = (column_ids[:, None] == jnp.arange(sub_count * slot_count)[None, :]).astype(
        jnp.float32
    )
    placer = jnp.dot(hit_counts, column_pick, precision=highest)
    gathered = jnp.dot(
        placer, incoming.reshape(device_count * slot_count, square), precision=highest
    )
    assembled = (
        gathered.reshape(row_blocks, col_blocks, BROWS, BROWS)
        .transpose(0, 2, 1, 3)
        .reshape(tile_rows, tile_cols)
    )
    global_rows = row_index * tile_rows + jnp.arange(tile_rows)
    global_cols = col_index * tile_cols + jnp.arange(tile_cols)
    on_diagonal = global_rows[:, None] == global_cols[None, :]
    matrix_tile = jnp.where(on_diagonal, interface_diag[:, None], 0.0) - assembled
    strip_rows = tile_rows // row_count
    strip_cols = tile_cols // col_count
    spread = matrix_tile.reshape(row_count, strip_rows, col_count, strip_cols)
    spread = exchange_both(spread, ("row", "col"), ("row", "col"), (0, 2), (0, 2))
    row_every = gathered_copies(row_scales, "row", 1)
    col_every = gathered_copies(col_scales, "col", 1)
    row_picked = lax.dynamic_slice_in_dim(
        row_every.reshape(2, row_count, tile_rows), row_index * strip_rows, strip_rows, 2
    )
    col_picked = lax.dynamic_slice_in_dim(
        col_every.reshape(2, col_count, tile_cols), col_index * strip_cols, strip_cols, 2
    )
    spread = mix_tile_rows(spread, row_picked[0], row_count // 4)
    spread = mix_tile_rows(spread, row_picked[1], row_count // 2)
    spread = mix_tile_cols(spread, col_picked[0], col_count // 4)
    spread = mix_tile_cols(spread, col_picked[1], col_count // 2)
    returned = exchange_both(spread, ("row", "col"), ("row", "col"), (0, 2), (0, 2))
    return returned.reshape(tile_rows, tile_cols)


def solution(mesh):
    in_specs = (
        P(("row", "col"), None, None),
        P(("row", "col"), None, None),
        P(("row", "col"), None, None),
        P(),
        P("row"),
        P(None, "row"),
        P(None, "col"),
    )
    out_specs = P("row", "col")
    return jax.shard_map(body, mesh=mesh, in_specs=in_specs, out_specs=out_specs, check_vma=False)
```

profile of v0, /device:TPU:1, one launch (start us, length us, event | category | flops | bytes accessed | tf_op | source)
XLA Modules:
  0.0 501.8 jit_solution(4270232051427710302)
XLA Ops:
  0.0 1.2 slice.63
  1.3 0.1 convert_reduce_fusion.1
  1.4 0.2 dynamic-slice_reduce_fusion.1
  1.6 0.2 dynamic-slice_reduce_fusion
  1.8 0.1 add_add_fusion.2
  1.9 0.1 add.147
  2.0 14.4 %fusion.2 = bf16[1024,2048]{1,0:T(8,128)(2,1)} fusion(bf16[1,2048,2048]{2,1,0:T(8,128)(2,1)} %param.8, bf16[1,1024,2048]{2,1,0:T(8,128)(2,1)} %param.7), kind=kOutput, calls=%fused_computation.7 | convolution fusion | flops 8589934592 | bytes 16777216 | tf_op jit(solution)/shard_map/dot_general | solution.py:88
  16.4 20.9 %fusion.18 = f32[128,8,8,128]{3,1,2,0:T(8,128)} fusion(bf16[1,2048,1024]{2,1,0:T(8,128)(2,1)} %param.9, bf16[1,2048,2048]{2,1,0:T(8,128)(2,1)} %param.8, bf16[1024,2048]{1,0:T(8,128)(2,1)} %fusion.2), kind=kOutput, calls=%fused_computation.28 | convolution fusion | flops 12886999040 | bytes 20971520 | tf_op jit(solution)/shard_map/dot_general | solution.py:97
  37.3 3.2 copy.72
  40.5 3.7 convolution_bitcast_fusion
  44.3 9.8 %copy.54 = f32[128,1,16384]{2,1,0:T(1,128)} copy(f32[128,1,16384]{2,0,1:T(8,128)S(1)} %convolution_bitcast_fusion) | data formatting | bytes 16777216 | tf_op jit(solution)/shard_map/reshape | solution.py:118
  54.1 0.0 copy-start.2
  54.1 11.9 %all-to-all-start = ((f32[128,1,16384]{2,1,0:T(1,128)}), f32[128,1,16384]{2,1,0:T(1,128)}, u32[]{:S(2)}, u32[]{:S(2)}) async-start(f32[128,1,16384]{2,1,0:T(1,128)} %copy.54), calls=%async_computation | async-start | bytes 16777216 | tf_op jit(solution)/shard_map/all_to_all | solution.py:121
  66.0 0.0 copy-done.2
  66.1 0.1 copy.53
  66.2 0.1 add.137
  66.3 1.7 convert_reduce_fusion
  68.0 4.8 copy.52
  72.8 0.0 copy-start
  72.8 6.9 %dot_general.24 = f32[16,8,1024]{2,1,0:T(8,128)S(1)} reshape(f32[128,128,8]{2,1,0:T(8,128)} %copy.52) | data formatting | bytes 1048576 | tf_op jit(solution)/shard_map/dot_general | solution.py:136
  79.8 0.5 convolution_bitcast_fusion.2
  80.3 86.2 %all-to-all-done = f32[128,1,16384]{2,1,0:T(1,128)} async-done(((f32[128,1,16384]{2,1,0:T(1,128)}), f32[128,1,16384]{2,1,0:T(1,128)}, u32[]{:S(2)}, u32[]{:S(2)}) %all-to-all-start) | async-done | bytes 8388640 | tf_op jit(solution)/shard_map/all_to_all | solution.py:121
  166.5 0.0 copy-done
  166.5 0.7 broadcast_in_dim.17
  167.2 5.7 %all-to-all-start.2 = ((f32[8,2,2048]{2,1,0:T(2,128)}), f32[8,2,2048]{2,1,0:T(2,128)S(1)}, u32[]{:S(2)}, u32[]{:S(2)}) async-start(f32[8,2,2048]{2,1,0:T(2,128)} %broadcast_in_dim.17), calls=%async_computation.2 | async-start | bytes 262144 | tf_op jit(solution)/shard_map/all_to_all | solution.py:37
  172.9 17.9 %copy.71 = f32[128,1,16384]{0,2,1:T(8,128)} copy(f32[128,1,16384]{2,1,0:T(1,128)} %all-to-all-done) | data formatting | bytes 16777216 | tf_op jit(solution)/shard_map/dot_general | solution.py:137
  190.8 12.0 %convolution_bitcast_fusion.1 = f32[16,128,8,128]{3,2,1,0:T(8,128)} fusion(f32[16,8,128,1]{2,1,3,0:T(8,128)S(1)} %convolution_bitcast_fusion.2, f32[128,128,128,1]{2,1,0,3:T(8,128)} %bitcast.125), kind=kOutput, calls=%fused_computation.27 | convolution fusion | flops 3221225472 | bytes 16842752 | tf_op jit(solution)/shard_map/dot_general | solution.py:137
  202.9 10.7 %copy.56 = f32[16,128,8,128]{1,0,3,2:T(8,128)} copy(f32[16,128,8,128]{3,2,1,0:T(8,128)} %convolution_bitcast_fusion.1) | data formatting | bytes 16777216 | tf_op jit(solution)/shard_map/transpose | solution.py:142
  213.6 0.0 copy-start.1
  213.6 9.8 %reshape.253 = f32[8,1,256,16,1,64]{2,0,5,3,4,1:T(8,128)} reshape(f32[16,128,8,128]{1,0,3,2:T(8,128)} %copy.56) | data formatting | bytes 16777216 | tf_op jit(solution)/shard_map/reshape | solution.py:143
  223.4 0.0 all-to-all-done.2
  223.4 0.0 copy-done.1
  223.4 0.7 broadcast_in_dim.18
  224.1 6.4 %all-to-all-start.3 = ((f32[16,2,1024]{2,1,0:T(2,128)}), f32[16,2,1024]{2,1,0:T(2,128)S(1)}, u32[]{:S(2)}, u32[]{:S(2)}) async-start(f32[16,2,1024]{2,1,0:T(2,128)} %broadcast_in_dim.18), calls=%async_computation.3 | async-start | bytes 262144 | tf_op jit(solution)/shard_map/all_to_all | solution.py:37
  230.5 4.7 subtract_bitcast_fusion
  235.2 6.0 %copy.57 = f32[8,16,1,256,1,64]{3,5,4,2,1,0:T(8,128)} copy(f32[8,16,1,256,1,64]{3,0,5,1,4,2:T(8,128)S(1)} %subtract_bitcast_fusion) | data formatting | bytes 16777216 | tf_op jit(solution)/shard_map/transpose;transpose | solution.py:27
  241.2 0.0 all-to-all-done.3
  241.2 9.3 %all-to-all-start.1 = ((f32[128,1,256,1,64]{2,4,3,1,0:T(8,128)}), f32[128,1,256,1,64]{2,4,3,1,0:T(8,128)}, u32[]{:S(2)}, u32[]{:S(2)}) async-start(f32[128,1,256,1,64]{2,4,3,1,0:T(8,128)} %bitcast.121), calls=%async_computation.1 | async-start | bytes 16777216 | tf_op jit(solution)/shard_map/all_to_all | solution.py:30
  250.6 0.1 constant_dynamic-slice_fusion
  250.7 99.9 %all-to-all-done.1 = f32[128,1,256,1,64]{2,4,3,1,0:T(8,128)} async-done(((f32[128,1,256,1,64]{2,4,3,1,0:T(8,128)}), f32[128,1,256,1,64]{2,4,3,1,0:T(8,128)}, u32[]{:S(2)}, u32[]{:S(2)}) %all-to-all-start.1) | async-done | bytes 8388640 | tf_op jit(solution)/shard_map/all_to_all | solution.py:30
  350.7 4.5 add_multiply_fusion.3
  355.2 1.8 maximum_multiply_fusion
  357.1 1.9 add_multiply_fusion.2
  358.9 1.8 maximum_multiply_fusion.1
  360.8 1.1 add_multiply_fusion.1
  361.9 1.8 maximum_multiply_fusion.2
  363.7 1.1 add_multiply_fusion
  364.9 1.8 maximum_multiply_fusion.3
  366.7 105.9 %all_to_all.25 = f32[128,1,256,1,64]{2,4,3,1,0:T(8,128)} all-to-all(f32[128,1,256,1,64]{2,4,3,1,0:T(8,128)S(1)} %bitcast.126), channel_id=1, replica_groups=mesh['row'=8,'col'=16] {'row','col'}, dimensions={0} | all-to-all | bytes 16777216 | tf_op jit(solution)/shard_map/all_to_all | solution.py:30
  472.6 14.5 %copy.62 = f32[8,256,16,1,64]{4,2,1,0,3:T(8,128)} copy(f32[8,256,16,1,64]{1,4,2,0,3:T(8,128)} %bitcast.120) | data formatting | bytes 16777216 | tf_op jit(solution)/shard_map/reshape;reshape | solution.py:166
  487.1 14.5 %reshape.263 = f32[2048,1024]{1,0:T(8,128)} reshape(f32[8,256,16,1,64]{4,2,1,0,3:T(8,128)} %copy.62) | data formatting | bytes 16777216 | tf_op jit(solution)/shard_map/reshape;reshape | solution.py:166
  (20 shorter events, 0.2 us)
Async XLA Ops:
  54.1 11.9 %copy-start.2 = (f32[2048]{0:T(1024)S(1)}, f32[2048]{0:T(1024)}, u32[]{:S(2)}) copy-start(f32[2048]{0:T(1024)} %param.11) | copy-start | bytes 24580
  54.1 112.4 %all-to-all-start = ((f32[128,1,16384]{2,1,0:T(1,128)}), f32[128,1,16384]{2,1,0:T(1,128)}, u32[]{:S(2)}, u32[]{:S(2)}) async-start(f32[128,1,16384]{2,1,0:T(1,128)} %copy.54), calls=%async_computation | async-start | bytes 16777216 | tf_op jit(solution)/shard_map/all_to_all | solution.py:121
  72.8 93.7 %copy-start = (f32[2,2048]{1,0:T(2,128)S(1)}, f32[2,2048]{1,0:T(2,128)}, u32[]{:S(2)}) copy-start(f32[2,2048]{1,0:T(2,128)} %param.12) | copy-start | bytes 49156
  167.2 56.2 %all-to-all-start.2 = ((f32[8,2,2048]{2,1,0:T(2,128)}), f32[8,2,2048]{2,1,0:T(2,128)S(1)}, u32[]{:S(2)}, u32[]{:S(2)}) async-start(f32[8,2,2048]{2,1,0:T(2,128)} %broadcast_in_dim.17), calls=%async_computation.2 | async-start | bytes 262144 | tf_op jit(solution)/shard_map/all_to_all | solution.py:37
  213.6 9.9 %copy-start.1 = (f32[2,1024]{1,0:T(2,128)S(1)}, f32[2,1024]{1,0:T(2,128)}, u32[]{:S(2)}) copy-start(f32[2,1024]{1,0:T(2,128)} %param.13) | copy-start | bytes 24580
  224.1 17.1 %all-to-all-start.3 = ((f32[16,2,1024]{2,1,0:T(2,128)}), f32[16,2,1024]{2,1,0:T(2,128)S(1)}, u32[]{:S(2)}, u32[]{:S(2)}) async-start(f32[16,2,1024]{2,1,0:T(2,128)} %broadcast_in_dim.18), calls=%async_computation.3 | async-start | bytes 262144 | tf_op jit(solution)/shard_map/all_to_all | solution.py:37
  241.2 109.5 %all-to-all-start.1 = ((f32[128,1,256,1,64]{2,4,3,1,0:T(8,128)}), f32[128,1,256,1,64]{2,4,3,1,0:T(8,128)}, u32[]{:S(2)}, u32[]{:S(2)}) async-start(f32[128,1,256,1,64]{2,4,3,1,0:T(8,128)} %bitcast.121), calls=%async_computation.1 | async-start | bytes 16777216 | tf_op jit(solution)/shard_map/all_to_all | solution.py:30
where the time goes:
time: 507 us; the launch traced here: 502 us
  waiting for transfers between devices  186 us (37%)
  blocking collectives  106 us (21%)
  local copies, waits for them, and re-layouts  101 us (20%)
  matrix products  51.6 us (10%)
  starting transfers between devices  33.4 us (7%)
  other arithmetic  22.9 us (5%)
    all_to_all x1, blocking collectives, exchange_both(): parts = lax.all_to_all(parts, axis, split_axis=0, concat_axis=0, tiled=True)  106 us
    all_to_all x1, waiting for transfers between devices, exchange_both(): parts = lax.all_to_all(parts, axis, split_axis=0, concat_axis=0, tiled=True)  99.9 us
    all_to_all x1, waiting for transfers between devices, body(): lax.all_to_all(outgoing, ('row', 'col'), split_axis=0, concat_axis=0, til...  86.2 us
    another operation x2, local copies, waits for them, and re-layouts, body(): return returned.reshape(tile_rows, tile_cols)  29 us
    dot_general x1, matrix products, body(): jnp.dot(left_part, right_part, preferred_element_type=jnp.float32)  20.9 us
    dot_general x1, local copies, waits for them, and re-layouts, body(): jnp.dot(placer, incoming.reshape(device_count * slot_count, square), prec...  17.9 us
    dot_general x1, matrix products, body(): lax.dot_general(coupling_left[0], inner_factor[0], (((1,), (1,)), ((), ()...  14.4 us
    all_to_all x2, starting transfers between devices, copy_for_each(): lax.all_to_all(jnp.broadcast_to(shard[None], (length, *shard.shape)), axi...  12.1 us
  transfers between devices with their start and end apart: 4, of which 2 were waited for; matrix products, arithmetic and copies ran while one was open for 15% of the time, Pallas kernels for 0%

commit v1 on v0

v1 whole, which is shorter than its diff:
```python
import functools

import jax
import jax.numpy as jnp
from jax import lax
from jax.experimental import pallas as pl
from jax.experimental.pallas import tpu as pltpu
from jax.sharding import PartitionSpec as P

MESH = pl.DeviceIdType.MESH
F32 = jnp.float32
BF16 = jnp.bfloat16

RUN = 128
INNER = 2048
CHUNK = 256
CHUNKS = INNER // CHUNK
PIECE = 32
PITCH = 40
SRC = 128
STRIPS = 32
TILE = 512
TILE_PITCH = 520
PCHUNK = 4
PSTEPS = 16 // PCHUNK


def position():
    row = lax.axis_index("row")
    col = lax.axis_index("col")
    return col // 4, row // 2, col % 4, row % 2


def device(x, y, z, core):
    return (y * 2 + core, x * 4 + z)


def kernel(
    left_hbm, factor_hbm, right_hbm, iface_hbm, diag_hbm, rows_hbm, cols_hbm,
    out_hbm,
    right_0, right_1, right_2, right_3, right_4, right_5, right_6, right_7, right_p, factor_v, left_v, mixed_v, lpart_v, send1, recv1, tiles, recv2, stage,
    iface_v, rows_v, diag_v, cols_v, cols8, iface_s, rows_s, diag_s,
    in_sem, small_sem, scale_send, scale_recv, send_sem1, zero_sem, recv_sem1, send_sem2, recv_sem2,
    out_sem,
):
    x, y, z, core = position()
    zp, zb = z // 2, z % 2
    me = (y * 2 + core) * 16 + x * 4 + z
    strip = (x * 4 + y) * 2 + zb

    barrier = pltpu.get_barrier_semaphore()

    def greet(o, carry):
        pl.semaphore_signal(
            barrier, inc=1, device_id=((y * 2 + core + o // 16) % 8, (x * 4 + z + o % 16) % 16),
            device_id_type=MESH,
        )
        return carry

    own_rows = pltpu.make_async_copy(
        iface_hbm.at[pl.ds(pl.multiple_of(me // 8 * 8, 8), 8), :], iface_s, small_sem.at[0]
    )
    own_rows.start()
    right_v = [right_0, right_1, right_2, right_3, right_4, right_5, right_6, right_7]
    factor_in = []
    for c in range(CHUNKS):
        rows = pl.ds(c * CHUNK, CHUNK)
        wide = pl.ds(0, (c + 1) * CHUNK)
        for k in range(8):
            pltpu.make_async_copy(
                right_hbm.at[0, rows, pl.ds(k * RUN, RUN)], right_v[c].at[k], in_sem.at[c]
            ).start()
        factor_in.append(
            pltpu.make_async_copy(
                factor_hbm.at[0, rows, wide], factor_v.at[rows, wide], in_sem.at[CHUNKS + c]
            )
        )
        factor_in[c].start()
    left_in = pltpu.make_async_copy(left_hbm, left_v, in_sem.at[2 * CHUNKS])
    left_in.start()
    iface_in = pltpu.make_async_copy(iface_hbm, iface_v, small_sem.at[1])
    iface_in.start()
    rows_in = pltpu.make_async_copy(rows_hbm, rows_v.at[y], small_sem.at[2])
    rows_in.start()
    diag_in = pltpu.make_async_copy(diag_hbm, diag_v.at[y], small_sem.at[3])
    diag_in.start()
    cols_in = pltpu.make_async_copy(cols_hbm, cols_v.at[x * 2 + zb], small_sem.at[4])
    cols_in.start()
    lax.fori_loop(1, SRC, greet, 0)
    own_rows.wait()

    run_tile = [lax.div(iface_s[me % 8, RUN * k], 16 * RUN) for k in range(8)]

    def run_in(j):
        found = jnp.int32(0)
        for k in range(1, 8):
            found += k * (run_tile[k] == j).astype(jnp.int32)
        return found & 7

    run_of = [run_in(j) for j in range(8)]

    for c in range(CHUNKS):
        rows = pl.ds(c * CHUNK, CHUNK)
        deep = (c + 1) * CHUNK
        pltpu.make_async_copy(right_v[c], right_v[c], in_sem.at[c]).wait()
        for m in range(8):
            right_p[rows, m * RUN : (m + 1) * RUN] = right_v[c][run_of[m]]
        factor_in[c].wait()
        mixed_v[rows, :] = jnp.dot(
            factor_v[rows, :deep], right_p[:deep, :], preferred_element_type=F32
        ).astype(BF16)
    left_in.wait()

    def send_group(g, carry):
        half, to_core = g // 2, g % 2
        runs = [run_in((half * 2 + y1) * 2 + to_core) for y1 in range(2)]
        for c in range(CHUNKS):
            rows = pl.ds(c * CHUNK, CHUNK)
            deep = (c + 1) * CHUNK
            taken = jnp.concatenate([left_v[run, :, :deep] for run in runs], axis=0)
            lpart_v[:, c * CHUNK : (c + 1) * CHUNK] = lax.dot_general(
                taken, factor_v[rows, :deep], (((1,), (1,)), ((), ())), preferred_element_type=F32
            ).astype(BF16)
        for pair in range(4):
            block = jnp.dot(
                lpart_v[...], mixed_v[:, pair * 2 * RUN : (pair + 1) * 2 * RUN],
                preferred_element_type=F32,
            )
            for half_pair in range(2):
                for y1 in range(2):
                    for i in range(4):
                        for t8 in range(4):
                            row = y1 * RUN + 32 * i + 8 * t8
                            base = (half_pair * 32 + 8 * t8) * PITCH + y1 * 16 + pair * 4 + i
                            send1[pl.ds(g * (64 * PITCH) + base, 8, stride=PITCH), :] = block[
                                row : row + 8, half_pair * RUN : (half_pair + 1) * RUN
                            ]

        @pl.when(g == 0)
        def _():
            pl.semaphore_wait(barrier, SRC - 1)

        def piece(px, py, pz):
            index = g * 64 + (pz // 2) * 32 + (px * 4 + py) * 2 + pz % 2
            return (
                send1.at[pl.ds(pl.multiple_of(index * PITCH, 8), PIECE), :],
                recv1.at[pl.ds(pl.multiple_of((half * SRC + me) * PITCH, 8), PIECE), :],
            )

        @pl.when(to_core == core)
        def _():
            src, dst = piece(x, y, z)
            pltpu.make_async_copy(src, dst, recv_sem1.at[half]).start()

        @pl.when(to_core != core)
        def _():
            src, dst = piece(x, y, z)
            pltpu.make_async_remote_copy(
                src, dst, zero_sem.at[half], recv_sem1.at[half],
                device_id=device(x, y, z, to_core), device_id_type=MESH,
            ).start()

        def one(o, inner):
            o = (o * 27) % 64
            px, py, pz = (x + o % 4) % 4, (y + o // 4 % 4) % 4, (z + o // 16) % 4
            src, dst = piece(px, py, pz)
            pltpu.make_async_remote_copy(
                src, dst, send_sem1.at[g], recv_sem1.at[half],
                device_id=device(px, py, pz, to_core), device_id_type=MESH,
            ).start()
            return inner

        lax.fori_loop(1, 64, one, 0)
        return carry

    lax.fori_loop(0, 4, send_group, 0)

    rows_in.wait()
    diag_in.wait()
    cols_in.wait()
    for d in range(1, 4):
        to = device(x, (y + d) % 4, z, core)
        pltpu.make_async_remote_copy(
            rows_v.at[y], rows_v.at[y], scale_send.at[d], scale_recv.at[d], device_id=to,
            device_id_type=MESH,
        ).start()
        pltpu.make_async_remote_copy(
            diag_v.at[y], diag_v.at[y], scale_send.at[3 + d], scale_recv.at[3 + d], device_id=to,
            device_id_type=MESH,
        ).start()
    for d in range(1, 8):
        pltpu.make_async_remote_copy(
            cols_v.at[x * 2 + zb], cols_v.at[x * 2 + zb], scale_send.at[6 + d],
            scale_recv.at[6 + d],
            device_id=device((x + d // 2) % 4, y, zp * 2 + (zb + d % 2) % 2, core),
            device_id_type=MESH,
        ).start()

    iface_in.wait()
    run_ids = []
    for k in range(8):
        run_ids.append(lax.div(iface_v[:, k * RUN : (k + 1) * RUN].T[0:1, :], RUN))

    def placed(j):
        total = jnp.zeros((1, SRC), jnp.int32)
        for k in range(8):
            total += jnp.where(run_ids[k] // 16 == j, run_ids[k] % 16, 0)
        return total

    col_place = [placed(2 * j + zp) for j in range(4)]
    row_place = [placed(2 * j + core) for j in range(4)]
    spots = lax.broadcasted_iota(jnp.int32, (256, SRC), 0)

    for half in range(2):
        got = recv1.at[pl.ds(0, SRC * PIECE), :]
        pltpu.make_async_copy(got, got, recv_sem1.at[half]).wait()
        for y1 in range(2):
            for xx in range(4):
                first = half * SRC * PITCH + y1 * 16 + xx * 4
                data = jnp.concatenate(
                    [recv1[pl.ds(first + i, SRC, stride=PITCH), :] for i in range(4)], axis=1
                )
                high = data.astype(BF16)
                low = (data - high.astype(F32)).astype(BF16)
                spot = row_place[half * 2 + y1] * 16 + col_place[xx]
                hot = jnp.where(spots == spot, -1.0, 0.0).astype(BF16)
                tile = jnp.dot(
                    jnp.concatenate([hot, hot], axis=1), jnp.concatenate([high, low], axis=0),
                    preferred_element_type=F32,
                )
                for zz in range(2):
                    base = (((half * 2 + y1) * 4 + xx) * 2 + zz) * TILE
                    for p in range(16):
                        for i in range(4):
                            tiles[base + p * 32 + i * 8 : base + p * 32 + i * 8 + 8, :] = tile[
                                p * 16 + zz * 8 : p * 16 + zz * 8 + 8, i * 128 : (i + 1) * 128
                            ]

    for d in range(1, 4):
        rows_v_any, diag_v_any = rows_v.at[y], diag_v.at[y]
        pltpu.make_async_remote_copy(
            rows_v_any, rows_v_any, scale_send.at[d], scale_recv.at[d],
            device_id=device(x, y, z, core), device_id_type=MESH,
        ).wait()
        pltpu.make_async_remote_copy(
            diag_v_any, diag_v_any, scale_send.at[3 + d], scale_recv.at[3 + d],
            device_id=device(x, y, z, core), device_id_type=MESH,
        ).wait()
    for d in range(1, 8):
        cols_any = cols_v.at[x * 2 + zb]
        pltpu.make_async_remote_copy(
            cols_any, cols_any, scale_send.at[6 + d], scale_recv.at[6 + d],
            device_id=device(x, y, z, core), device_id_type=MESH,
        ).wait()
    rows_to = pltpu.make_async_copy(rows_v, rows_s, small_sem.at[2])
    diag_to = pltpu.make_async_copy(diag_v, diag_s, small_sem.at[3])
    rows_to.start()
    diag_to.start()
    for xz in range(8):
        for level in range(2):
            for q in range(8):
                cols8[xz, level, q : q + 1, :] = cols_v[
                    xz, level : level + 1, q * 128 : (q + 1) * 128
                ] * (1.0 if level == 0 else 0.25)
    rows_to.wait()
    diag_to.wait()

    sub8 = lax.broadcasted_iota(jnp.int32, (8, 128), 0)
    lane8 = lax.broadcasted_iota(jnp.int32, (8, 128), 1)

    for step in range(PSTEPS):

        def mix(pp, carry):
            p = step * PCHUNK + pp
            for zz in range(2):
                first = [cols8[xx * 2 + zz, 0] for xx in range(4)]
                second = [cols8[xx * 2 + zz, 1] for xx in range(4)]
                for i in range(4):
                    spot = p * RUN + 32 * i + strip
                    on = (sub8 + 8 * zz == p) & (lane8 == 32 * i + strip) & (core == zp)

                    def at(yy, xx):
                        start = ((yy * 4 + xx) * 2 + zz) * TILE + p * 32 + i * 8
                        return pl.ds(pl.multiple_of(start, 8), 8)

                    s0 = [rows_s[yy, 0, spot] for yy in range(4)]
                    s1 = [rows_s[yy, 1, spot] for yy in range(4)]
                    held = [[None] * 4 for _ in range(4)]
                    for xx in range(4):
                        a = [tiles[at(yy, xx), :] for yy in range(4)]
                        a[xx] = a[xx] + jnp.where(on, diag_s[xx, 0, spot], 0.0)
                        b0, b1 = (a[0] + a[1]) * s0[0], (a[0] - a[1]) * s0[1]
                        b2, b3 = (a[2] + a[3]) * s0[2], (a[2] - a[3]) * s0[3]
                        held[0][xx] = (b0 + b2) * s1[0]
                        held[2][xx] = (b0 - b2) * s1[2]
                        held[1][xx] = (b1 + b3) * s1[1]
                        held[3][xx] = (b1 - b3) * s1[3]
                    for yy in range(4):
                        a = held[yy]
                        b0, b1 = (a[0] + a[1]) * first[0], (a[0] - a[1]) * first[1]
                        b2, b3 = (a[2] + a[3]) * first[2], (a[2] - a[3]) * first[3]
                        tiles[at(yy, 0), :] = (b0 + b2) * second[0]
                        tiles[at(yy, 2), :] = (b0 - b2) * second[2]
                        tiles[at(yy, 1), :] = (b1 + b3) * second[1]
                        tiles[at(yy, 3), :] = (b1 - b3) * second[3]
            return carry

        lax.fori_loop(0, PCHUNK, mix, 0)

        def back(px, py, pzb):
            index = (py * 4 + px) * 2 + pzb
            return (
                tiles.at[pl.ds(pl.multiple_of(index * TILE + step * PCHUNK * 32, 8), PCHUNK * 32), :],
                recv2.at[
                    pl.ds(pl.multiple_of(strip * TILE_PITCH + step * PCHUNK * 32, 8), PCHUNK * 32), :
                ],
            )

        src, dst = back(x, y, zb)
        pltpu.make_async_copy(src, dst, recv_sem2.at[step]).start()

        def one_back(o, carry):
            o = (o * 11) % 32
            px, py, pzb = (x + o % 4) % 4, (y + o // 4 % 4) % 4, (zb + o // 16) % 2
            src, dst = back(px, py, pzb)
            pltpu.make_async_remote_copy(
                src, dst, send_sem2.at[step], recv_sem2.at[step],
                device_id=device(px, py, zp * 2 + pzb, core), device_id_type=MESH,
            ).start()
            return carry

        lax.fori_loop(1, STRIPS, one_back, 0)

    def put(p, slot):
        return pltpu.make_async_copy(
            stage.at[slot], out_hbm.at[pl.ds(pl.multiple_of(p * RUN, RUN), RUN), :], out_sem.at[slot]
        )

    for step in range(PSTEPS):
        got = recv2.at[pl.ds(0, STRIPS * PCHUNK * 32), :]
        pltpu.make_async_copy(got, got, recv_sem2.at[step]).wait()
        for pp in range(PCHUNK):
            p = step * PCHUNK + pp
            slot = p % 4
            if p >= 4:
                put(p - 4, slot).wait()

            def merge(i, carry):
                for a in range(4):
                    for q in range(8):
                        stage[
                            slot, pl.ds(pl.multiple_of(32 * i + 8 * a, 8), 8), q * 128 : (q + 1) * 128
                        ] = recv2[
                            pl.ds(8 * a * TILE_PITCH + p * 32 + i * 8 + q, 8, stride=TILE_PITCH), :
                        ]
                return carry

            lax.fori_loop(0, 4, merge, 0)
            put(p, slot).start()
    for p in range(12, 16):
        put(p, p % 4).wait()

    for g in range(4):
        sent = send1.at[pl.ds(0, 63 * PIECE), :]
        pltpu.make_async_copy(sent, sent, send_sem1.at[g]).wait()
    for half in range(2):
        sent = send1.at[pl.ds(0, PIECE), :]
        pltpu.make_async_copy(sent, sent, zero_sem.at[half]).wait()
    for step in range(PSTEPS):
        sent = tiles.at[pl.ds(0, (STRIPS - 1) * PCHUNK * 32), :]
        pltpu.make_async_copy(sent, sent, send_sem2.at[step]).wait()


def body(
    coupling_left, inner_factor, coupling_right, iface_rows, interface_diag, row_scales, col_scales
):
    any_space = pl.BlockSpec(memory_space=pl.ANY)
    return pl.pallas_call(
        kernel,
        out_shape=jax.ShapeDtypeStruct((2048, 1024), F32),
        in_specs=[any_space] * 7,
        out_specs=any_space,
        scratch_shapes=[
            *[pltpu.VMEM((8, CHUNK, RUN), BF16)] * CHUNKS,
            pltpu.VMEM((INNER, 1024), BF16),
            pltpu.VMEM((INNER, INNER), BF16),
            pltpu.VMEM((8, RUN, INNER), BF16),
            pltpu.VMEM((INNER, 1024), BF16),
            pltpu.VMEM((2 * RUN, INNER), BF16),
            pltpu.VMEM((4 * 64 * PITCH, 128), F32),
            pltpu.VMEM((2 * SRC * PITCH, 128), F32),
            pltpu.VMEM((STRIPS * TILE, 128), F32),
            pltpu.VMEM((STRIPS * TILE_PITCH, 128), F32),
            pltpu.VMEM((4, RUN, 1024), F32),
            pltpu.VMEM((SRC, 1024), jnp.int32),
            pltpu.VMEM((4, 2, 2048), F32),
            pltpu.VMEM((4, 1, 2048), F32),
            pltpu.VMEM((8, 2, 1024), F32),
            pltpu.VMEM((8, 2, 8, 128), F32),
            pltpu.SMEM((8, 1024), jnp.int32),
            pltpu.SMEM((4, 2, 2048), F32),
            pltpu.SMEM((4, 1, 2048), F32),
            pltpu.SemaphoreType.DMA((2 * CHUNKS + 1,)),
            pltpu.SemaphoreType.DMA((5,)),
            pltpu.SemaphoreType.DMA((14,)),
            pltpu.SemaphoreType.DMA((14,)),
            pltpu.SemaphoreType.DMA((4,)),
            pltpu.SemaphoreType.DMA((2,)),
            pltpu.SemaphoreType.DMA((2,)),
            pltpu.SemaphoreType.DMA((PSTEPS,)),
            pltpu.SemaphoreType.DMA((PSTEPS,)),
            pltpu.SemaphoreType.DMA((4,)),
        ],
        compiler_params=pltpu.CompilerParams(
            collective_id=0, has_side_effects=True, vmem_limit_bytes=63 * 2**20
        ),
    )(
        coupling_left.reshape(8, RUN, INNER), inner_factor, coupling_right, iface_rows, interface_diag[None, :],
        row_scales, col_scales,
    )


def solution(mesh):
    in_specs = (
        P(("row", "col"), None, None),
        P(("row", "col"), None, None),
        P(("row", "col"), None, None),
        P(),
        P("row"),
        P(None, "row"),
        P(None, "col"),
    )
    out_specs = P("row", "col")
    return jax.shard_map(body, mesh=mesh, in_specs=in_specs, out_specs=out_specs, check_vma=False)
```

time: 507 us -> 186 us (0.37)
  the two profiles are of different devices: /device:TPU:1 before, /device:TPU:67 now
where the time goes in v1:
time: 186 us
  Pallas kernels  177 us (95%)
  local copies, waits for them, and re-layouts  8.44 us (5%)
    pallas_call x1, Pallas kernels, body(): pl.pallas_call(kernel, out_shape=jax.ShapeDtypeStruct((2048, 1024), F32),...  177 us
    unnamed x1, local copies, waits for them, and re-layouts  8.44 us

profile of v1, /device:TPU:67, one launch (start us, length us, event | category | flops | bytes accessed | tf_op | source)
XLA Modules:
  0.0 185.6 jit_solution(5917560522713468203)
XLA Ops:
  0.0 177.2 %shard_map.73 = f32[2048,1024]{1,0:T(8,128)} custom-call(bf16[8,128,2048]{2,1,0:T(8,128)(2,1)} %bitcast.2, bf16[1,2048,2048]{2,1,0:T(8,128)(2,1)} %factor_hbm.1, bf16[1,2048,1024]{2,1,0:T(8,128)(2,1)} %right_hbm.1, s32[128,1024]{1,0:T(8,128)} %iface_hbm.1, f32[1,2048]{1,0:T(1,128)} %bitcast.3, f32[2,2048]{1,0:T(2,128)} %rows_hbm.1, f32[2,1024]{1,0:T(2,128)} %cols_hbm.1), custom_call_target="tpu_custom_call" | custom-call | tf_op jit(solution)/shard_map/pallas_call | solution.py:378
  177.2 8.4 %copy.9 = f32[2048,1024]{1,0:T(8,128)} copy(f32[2048,1024]{1,0:T(8,128)} %shard_map.73) | data formatting | bytes 16777216

commit v2 on v1

v2 whole, which is shorter than its diff:
```python
import functools

import jax
import jax.numpy as jnp
from jax import lax
from jax.experimental import pallas as pl
from jax.experimental.pallas import tpu as pltpu
from jax.sharding import PartitionSpec as P

MESH = pl.DeviceIdType.MESH
F32 = jnp.float32
BF16 = jnp.bfloat16

VLIM = 63 * 2**20
RUN = 128
INNER = 2048
CHUNK = 256
CHUNKS = INNER // CHUNK
PIECE = 32
PITCH = 40
SRC = 128
STRIPS = 32
TILE = 512
TILE_PITCH = 512
SET = TILE // 2
PCHUNK = 8
PSTEPS = 16 // PCHUNK


def position():
    row = lax.axis_index("row")
    col = lax.axis_index("col")
    return col // 4, row // 2, col % 4, row % 2


def device(x, y, z, core):
    return (y * 2 + core, x * 4 + z)


def kernel(
    left_hbm, factor_hbm, right_hbm, iface_hbm, diag_hbm, rows_hbm, cols_hbm,
    recv2,
    right_0, right_1, right_2, right_3, right_4, right_5, right_6, right_7, right_p, factor_v, left_v, mixed_v, lpart_v, send1, recv1, tiles,
    iface_v, rows_v, diag_v, cols_v, cols8, iface_s, rows_s, diag_s,
    in_sem, small_sem, scale_send, scale_recv, send_sem1, zero_sem, recv_sem1, send_sem2, recv_sem2,
):
    x, y, z, core = position()
    zp, zb = z // 2, z % 2
    me = (y * 2 + core) * 16 + x * 4 + z
    strip = (x * 4 + y) * 2 + zb

    barrier = pltpu.get_barrier_semaphore()

    def greet(o, carry):
        pl.semaphore_signal(
            barrier, inc=1, device_id=((y * 2 + core + o // 16) % 8, (x * 4 + z + o % 16) % 16),
            device_id_type=MESH,
        )
        return carry

    own_rows = pltpu.make_async_copy(
        iface_hbm.at[pl.ds(pl.multiple_of(me // 8 * 8, 8), 8), :], iface_s, small_sem.at[0]
    )
    own_rows.start()
    right_v = [right_0, right_1, right_2, right_3, right_4, right_5, right_6, right_7]
    factor_in = []
    for c in range(CHUNKS):
        rows = pl.ds(c * CHUNK, CHUNK)
        wide = pl.ds(0, (c + 1) * CHUNK)
        for k in range(8):
            pltpu.make_async_copy(
                right_hbm.at[0, rows, pl.ds(k * RUN, RUN)], right_v[c].at[k], in_sem.at[c]
            ).start()
        factor_in.append(
            pltpu.make_async_copy(
                factor_hbm.at[0, rows, wide], factor_v.at[rows, wide], in_sem.at[CHUNKS + c]
            )
        )
        factor_in[c].start()
    left_in = pltpu.make_async_copy(left_hbm, left_v, in_sem.at[2 * CHUNKS])
    left_in.start()
    iface_in = pltpu.make_async_copy(iface_hbm, iface_v, small_sem.at[1])
    iface_in.start()
    rows_in = pltpu.make_async_copy(rows_hbm, rows_v.at[y], small_sem.at[2])
    rows_in.start()
    diag_in = pltpu.make_async_copy(diag_hbm, diag_v.at[y], small_sem.at[3])
    diag_in.start()
    cols_in = pltpu.make_async_copy(cols_hbm, cols_v.at[x * 2 + zb], small_sem.at[4])
    cols_in.start()
    lax.fori_loop(1, SRC, greet, 0)
    own_rows.wait()

    run_tile = [lax.div(iface_s[me % 8, RUN * k], 16 * RUN) for k in range(8)]

    def run_in(j):
        found = jnp.int32(0)
        for k in range(1, 8):
            found += k * (run_tile[k] == j).astype(jnp.int32)
        return found & 7

    run_of = [run_in(j) for j in range(8)]

    for c in range(CHUNKS):
        rows = pl.ds(c * CHUNK, CHUNK)
        deep = (c + 1) * CHUNK
        pltpu.make_async_copy(right_v[c], right_v[c], in_sem.at[c]).wait()
        for m in range(8):
            right_p[rows, m * RUN : (m + 1) * RUN] = right_v[c][run_of[m]]
        factor_in[c].wait()
        mixed_v[rows, :] = jnp.dot(
            factor_v[rows, :deep], right_p[:deep, :], preferred_element_type=F32
        ).astype(BF16)
    left_in.wait()

    def send_group(g, carry):
        half, to_core = g // 2, g % 2
        runs = [run_in((half * 2 + y1) * 2 + to_core) for y1 in range(2)]
        for c in range(CHUNKS):
            rows = pl.ds(c * CHUNK, CHUNK)
            deep = (c + 1) * CHUNK
            taken = jnp.concatenate([left_v[run, :, :deep] for run in runs], axis=0)
            lpart_v[:, c * CHUNK : (c + 1) * CHUNK] = lax.dot_general(
                taken, factor_v[rows, :deep], (((1,), (1,)), ((), ())), preferred_element_type=F32
            ).astype(BF16)
        for pair in range(4):
            block = jnp.dot(
                lpart_v[...], mixed_v[:, pair * 2 * RUN : (pair + 1) * 2 * RUN],
                preferred_element_type=F32,
            )
            for half_pair in range(2):
                for y1 in range(2):
                    slot = y1 * 4 + pair
                    for b in range(16):
                        base = ((b // 8) * 4 * 64 + half_pair * 32 + 4 * (b % 8)) * 16 + slot
                        send1[pl.ds((to_core * 2 + half) * (64 * 16) + base, 8, stride=8), :] = block[
                            y1 * RUN + 8 * b : y1 * RUN + 8 * b + 8,
                            half_pair * RUN : (half_pair + 1) * RUN,
                        ]

        @pl.when(g == 0)
        def _():
            pl.semaphore_wait(barrier, SRC - 1)
            rows_in.wait()
            diag_in.wait()
            cols_in.wait()
            for d in range(1, 4):
                to = device(x, (y + d) % 4, z, core)
                pltpu.make_async_remote_copy(
                    rows_v.at[y], rows_v.at[y], scale_send.at[d], scale_recv.at[d], device_id=to,
                    device_id_type=MESH,
                ).start()
                pltpu.make_async_remote_copy(
                    diag_v.at[y], diag_v.at[y], scale_send.at[3 + d], scale_recv.at[3 + d], device_id=to,
                    device_id_type=MESH,
                ).start()
            for d in range(1, 8):
                pltpu.make_async_remote_copy(
                    cols_v.at[x * 2 + zb], cols_v.at[x * 2 + zb], scale_send.at[6 + d],
                    scale_recv.at[6 + d],
                    device_id=device((x + d // 2) % 4, y, zp * 2 + (zb + d % 2) % 2, core),
                    device_id_type=MESH,
                ).start()

        send_pieces(0, to_core, half, send_sem1.at[g], zero_sem.at[half])
        return carry

    def send_pieces(part, to_core, half, sent, sent_zero):
        def piece(px, py, pz):
            index = (part * 4 + to_core * 2 + half) * 64 + (pz // 2) * 32
            index += (px * 4 + py) * 2 + pz % 2
            return (
                send1.at[pl.ds(pl.multiple_of(index * 16, 8), 16), :],
                recv1.at[pl.ds(pl.multiple_of((part * SRC + me) * PITCH + half * 16, 8), 16), :],
            )

        @pl.when(to_core == core)
        def _():
            src, dst = piece(x, y, z)
            pltpu.make_async_copy(src, dst, recv_sem1.at[part]).start()

        @pl.when(to_core != core)
        def _():
            src, dst = piece(x, y, z)
            pltpu.make_async_remote_copy(
                src, dst, sent_zero, recv_sem1.at[part],
                device_id=device(x, y, z, to_core), device_id_type=MESH,
            ).start()

        def one(o, inner):
            o = (o * 27) % 64
            px, py, pz = (x + o % 4) % 4, (y + o // 4 % 4) % 4, (z + o // 16) % 4
            src, dst = piece(px, py, pz)
            pltpu.make_async_remote_copy(
                src, dst, sent, recv_sem1.at[part],
                device_id=device(px, py, pz, to_core), device_id_type=MESH,
            ).start()
            return inner

        lax.fori_loop(1, 64, one, 0)

    lax.fori_loop(0, 4, send_group, 0)

    def send_rest(g, carry):
        send_pieces(1, g % 2, g // 2, send_sem1.at[4 + g], zero_sem.at[2 + g // 2])
        return carry

    lax.fori_loop(0, 4, send_rest, 0)

    iface_in.wait()
    run_ids = []
    for k in range(8):
        run_ids.append(lax.div(iface_v[:, k * RUN : (k + 1) * RUN].T[0:1, :], RUN))

    def placed(j):
        total = jnp.zeros((1, SRC), jnp.int32)
        for k in range(8):
            total += jnp.where(run_ids[k] // 16 == j, run_ids[k] % 16, 0)
        return total

    col_place = [placed(2 * j + zp) for j in range(4)]
    row_place = [placed(2 * j + core) for j in range(4)]
    spots = lax.broadcasted_iota(jnp.int32, (256, SRC), 0)

    def place(part):
        got = recv1.at[pl.ds(0, SRC * PIECE), :]
        pltpu.make_async_copy(got, got, recv_sem1.at[part]).wait()
        for yy in range(4):
            for xx in range(4):
                first = part * SRC * PITCH + (yy // 2) * 16 + (yy % 2) * 4 + xx
                data = jnp.concatenate(
                    [recv1[pl.ds(first + 8 * i, SRC, stride=PITCH), :] for i in range(2)], axis=1
                )
                high = data.astype(BF16)
                low = (data - high.astype(F32)).astype(BF16)
                spot = row_place[yy] * 16 + col_place[xx]
                hot = jnp.where(spots == spot, -1.0, 0.0).astype(BF16)
                tile = jnp.dot(
                    jnp.concatenate([hot, hot], axis=1), jnp.concatenate([high, low], axis=0),
                    preferred_element_type=F32,
                )
                for zz in range(2):
                    base = ((yy * 4 + xx) * 2 + zz) * TILE + part * SET
                    for p in range(16):
                        for i in range(2):
                            tiles[pl.ds(base + p * 16 + i, 8, stride=2), :] = tile[
                                p * 16 + zz * 8 : p * 16 + zz * 8 + 8, i * 128 : (i + 1) * 128
                            ]

    place(0)
    for d in range(1, 4):
        rows_v_any, diag_v_any = rows_v.at[y], diag_v.at[y]
        pltpu.make_async_remote_copy(
            rows_v_any, rows_v_any, scale_send.at[d], scale_recv.at[d],
            device_id=device(x, y, z, core), device_id_type=MESH,
        ).wait()
        pltpu.make_async_remote_copy(
            diag_v_any, diag_v_any, scale_send.at[3 + d], scale_recv.at[3 + d],
            device_id=device(x, y, z, core), device_id_type=MESH,
        ).wait()
    for d in range(1, 8):
        cols_any = cols_v.at[x * 2 + zb]
        pltpu.make_async_remote_copy(
            cols_any, cols_any, scale_send.at[6 + d], scale_recv.at[6 + d],
            device_id=device(x, y, z, core), device_id_type=MESH,
        ).wait()
    rows_to = pltpu.make_async_copy(rows_v, rows_s, small_sem.at[2])
    diag_to = pltpu.make_async_copy(diag_v, diag_s, small_sem.at[3])
    rows_to.start()
    diag_to.start()
    for xz in range(8):
        for level in range(2):
            for q in range(8):
                cols8[xz, level, q // 4, q % 4 * 2 : q % 4 * 2 + 2, :] = jnp.broadcast_to(
                    cols_v[xz, level : level + 1, q * 128 : (q + 1) * 128]
                    * (1.0 if level == 0 else 0.25),
                    (2, 128),
                )
    rows_to.wait()
    diag_to.wait()

    sub8 = lax.broadcasted_iota(jnp.int32, (8, 128), 0)
    lane8 = lax.broadcasted_iota(jnp.int32, (8, 128), 1)
    odd = sub8 % 2 == 1

    def mix_and_send(part, step):

        def mix(pp, carry):
            p = step * PCHUNK + pp
            within = 64 * part + 2 * strip
            spot = p * RUN + within
            s0 = [jnp.where(odd, rows_s[yy, 0, spot + 1], rows_s[yy, 0, spot]) for yy in range(4)]
            s1 = [jnp.where(odd, rows_s[yy, 1, spot + 1], rows_s[yy, 1, spot]) for yy in range(4)]
            diags = [
                jnp.where(odd, diag_s[yy, 0, spot + 1], diag_s[yy, 0, spot]) for yy in range(4)
            ]
            for zz in range(2):
                for h in range(2):
                    first = [cols8[xx * 2 + zz, 0, h] for xx in range(4)]
                    second = [cols8[xx * 2 + zz, 1, h] for xx in range(4)]
                    on = (sub8 // 2 + 8 * zz + 4 * h == p) & (lane8 == within + sub8 % 2)
                    on = on & (core == zp)

                    def at(yy, xx):
                        start = ((yy * 4 + xx) * 2 + zz) * TILE + part * SET + p * 16 + h * 8
                        return pl.ds(pl.multiple_of(start, 8), 8)

                    held = [[None] * 4 for _ in range(4)]
                    for xx in range(4):
                        a = [tiles[at(yy, xx), :] for yy in range(4)]
                        a[xx] = a[xx] + jnp.where(on, diags[xx], 0.0)
                        b0, b1 = (a[0] + a[1]) * s0[0], (a[0] - a[1]) * s0[1]
                        b2, b3 = (a[2] + a[3]) * s0[2], (a[2] - a[3]) * s0[3]
                        held[0][xx] = (b0 + b2) * s1[0]
                        held[2][xx] = (b0 - b2) * s1[2]
                        held[1][xx] = (b1 + b3) * s1[1]
                        held[3][xx] = (b1 - b3) * s1[3]
                    for yy in range(4):
                        a = held[yy]
                        b0, b1 = (a[0] + a[1]) * first[0], (a[0] - a[1]) * first[1]
                        b2, b3 = (a[2] + a[3]) * first[2], (a[2] - a[3]) * first[3]
                        tiles[at(yy, 0), :] = (b0 + b2) * second[0]
                        tiles[at(yy, 2), :] = (b0 - b2) * second[2]
                        tiles[at(yy, 1), :] = (b1 + b3) * second[1]
                        tiles[at(yy, 3), :] = (b1 - b3) * second[3]
            return carry

        lax.fori_loop(0, PCHUNK, mix, 0)

        chunk = part * SET + step * PCHUNK * 16

        def back(px, py, pzb):
            index = (py * 4 + px) * 2 + pzb
            return (
                tiles.at[pl.ds(pl.multiple_of(index * TILE + chunk, 8), PCHUNK * 16), :],
                recv2.at[pl.ds(pl.multiple_of(strip * TILE_PITCH + chunk, 8), PCHUNK * 16), :],
            )

        src, dst = back(x, y, zb)
        order = part * PSTEPS + step
        pltpu.make_async_copy(src, dst, recv_sem2.at[order]).start()

        def one_back(o, carry):
            o = (o * 11) % 32
            px, py, pzb = (x + o % 4) % 4, (y + o // 4 % 4) % 4, (zb + o // 16) % 2
            src, dst = back(px, py, pzb)
            pltpu.make_async_remote_copy(
                src, dst, send_sem2.at[order], recv_sem2.at[order],
                device_id=device(px, py, zp * 2 + pzb, core), device_id_type=MESH,
            ).start()
            return carry

        lax.fori_loop(1, STRIPS, one_back, 0)

    for step in range(PSTEPS):
        mix_and_send(0, step)
    place(1)
    for step in range(PSTEPS):
        mix_and_send(1, step)

    for order in range(2 * PSTEPS):
        got = recv2.at[pl.ds(0, STRIPS * PCHUNK * 16), :]
        pltpu.make_async_copy(got, got, recv_sem2.at[order]).wait()

    for g in range(8):
        sent = send1.at[pl.ds(0, 63 * 16), :]
        pltpu.make_async_copy(sent, sent, send_sem1.at[g]).wait()
    for half in range(2):
        sent = send1.at[pl.ds(0, 16), :]
        pltpu.make_async_copy(sent, sent, zero_sem.at[half]).wait()
        sent = send1.at[pl.ds(0, 16), :]
        pltpu.make_async_copy(sent, sent, zero_sem.at[2 + half]).wait()
    for order in range(2 * PSTEPS):
        sent = tiles.at[pl.ds(0, (STRIPS - 1) * PCHUNK * 16), :]
        pltpu.make_async_copy(sent, sent, send_sem2.at[order]).wait()


def merge(strips, out, got, held, in_sem, out_sem):
    sub8 = lax.broadcasted_iota(jnp.int32, (8, 128), 0)
    upper = sub8 < 4
    even = sub8 // 2 % 2 == 0

    def fetch(p, part):
        return pltpu.make_async_copy(
            strips.at[:, pl.ds(pl.multiple_of(part * SET + p * 16, 8), 16), :],
            got.at[p, part], in_sem.at[p],
        )

    def put(p):
        return pltpu.make_async_copy(
            held.at[p], out.at[pl.ds(pl.multiple_of(p * RUN, RUN), RUN), :], out_sem.at[p]
        )

    def start(p, carry):
        for part in range(2):
            fetch(p, part).start()
        return carry

    lax.fori_loop(0, 16, start, 0)

    def swap(a, b, mask, shift):
        return (
            jnp.where(mask, a, pltpu.roll(b, shift, 0)),
            jnp.where(mask, pltpu.roll(a, 8 - shift, 0), b),
        )

    def one(p, carry):
        pltpu.make_async_copy(got.at[p], got.at[p], in_sem.at[p]).wait()
        for part in range(2):
            for a in range(8):
                for h in range(2):
                    v = [got[p, part, 4 * a + k, 8 * h : 8 * h + 8, :] for k in range(4)]
                    v[0], v[2] = swap(v[0], v[2], upper, 4)
                    v[1], v[3] = swap(v[1], v[3], upper, 4)
                    v[0], v[1] = swap(v[0], v[1], even, 2)
                    v[2], v[3] = swap(v[2], v[3], even, 2)
                    for k in range(4):
                        q = 4 * h + k
                        held[
                            p, 64 * part + 8 * a : 64 * part + 8 * a + 8, q * 128 : (q + 1) * 128
                        ] = v[k]
        put(p).start()
        return carry

    lax.fori_loop(0, 16, one, 0)

    def finish(p, carry):
        put(p).wait()
        return carry

    lax.fori_loop(0, 16, finish, 0)


def body(
    coupling_left, inner_factor, coupling_right, iface_rows, interface_diag, row_scales, col_scales
):
    any_space = pl.BlockSpec(memory_space=pl.ANY)
    strips = pl.pallas_call(
        kernel,
        out_shape=jax.ShapeDtypeStruct((STRIPS * TILE_PITCH, 128), F32),
        in_specs=[any_space] * 7,
        out_specs=any_space,
        scratch_shapes=[
            *[pltpu.VMEM((8, CHUNK, RUN), BF16)] * CHUNKS,
            pltpu.VMEM((INNER, 1024), BF16),
            pltpu.VMEM((INNER, INNER), BF16),
            pltpu.VMEM((8, RUN, INNER), BF16),
            pltpu.VMEM((INNER, 1024), BF16),
            pltpu.VMEM((2 * RUN, INNER), BF16),
            pltpu.VMEM((2 * 4 * 64 * 16, 128), F32),
            pltpu.VMEM((2 * SRC * PITCH, 128), F32),
            pltpu.VMEM((STRIPS * TILE, 128), F32),
            pltpu.VMEM((SRC, 1024), jnp.int32),
            pltpu.VMEM((4, 2, 2048), F32),
            pltpu.VMEM((4, 1, 2048), F32),
            pltpu.VMEM((8, 2, 1024), F32),
            pltpu.VMEM((8, 2, 2, 8, 128), F32),
            pltpu.SMEM((8, 1024), jnp.int32),
            pltpu.SMEM((4, 2, 2048), F32),
            pltpu.SMEM((4, 1, 2048), F32),
            pltpu.SemaphoreType.DMA((2 * CHUNKS + 1,)),
            pltpu.SemaphoreType.DMA((5,)),
            pltpu.SemaphoreType.DMA((14,)),
            pltpu.SemaphoreType.DMA((14,)),
            pltpu.SemaphoreType.DMA((8,)),
            pltpu.SemaphoreType.DMA((4,)),
            pltpu.SemaphoreType.DMA((2,)),
            pltpu.SemaphoreType.DMA((2 * PSTEPS,)),
            pltpu.SemaphoreType.DMA((2 * PSTEPS,)),
        ],
        compiler_params=pltpu.CompilerParams(
            collective_id=0, has_side_effects=True, vmem_limit_bytes=VLIM
        ),
    )(
        coupling_left.reshape(8, RUN, INNER), inner_factor, coupling_right, iface_rows, interface_diag[None, :],
        row_scales, col_scales,
    )
    return pl.pallas_call(
        merge,
        out_shape=jax.ShapeDtypeStruct((2048, 1024), F32),
        in_specs=[any_space],
        out_specs=any_space,
        scratch_shapes=[
            pltpu.VMEM((16, 2, STRIPS, 16, 128), F32),
            pltpu.VMEM((16, RUN, 1024), F32),
            pltpu.SemaphoreType.DMA((16,)),
            pltpu.SemaphoreType.DMA((16,)),
        ],
        compiler_params=pltpu.CompilerParams(vmem_limit_bytes=63 * 2**20),
    )(strips.reshape(STRIPS, TILE_PITCH, 128))


def solution(mesh):
    in_specs = (
        P(("row", "col"), None, None),
        P(("row", "col"), None, None),
        P(("row", "col"), None, None),
        P(),
        P("row"),
        P(None, "row"),
        P(None, "col"),
    )
    out_specs = P("row", "col")
    return jax.shard_map(body, mesh=mesh, in_specs=in_specs, out_specs=out_specs, check_vma=False)
```

time: 186 us -> 168 us (0.903)
  the two profiles are of different devices: /device:TPU:67 before, /device:TPU:1 now
where the time goes in v2:
time: 168 us; the launch traced here: 167 us
  Pallas kernels  167 us (99%)
    pallas_call x1, Pallas kernels, body(): pl.pallas_call(kernel, out_shape=jax.ShapeDtypeStruct((STRIPS * TILE_PITC...  160 us
    pallas_call x1, Pallas kernels, body(): pl.pallas_call(merge, out_shape=jax.ShapeDtypeStruct((2048, 1024), F32),...  6.62 us

profile of v2, /device:TPU:1, one launch (start us, length us, event | category | flops | bytes accessed | tf_op | source)
XLA Modules:
  0.0 166.8 jit_solution(7683818670818238418)
XLA Ops:
  0.0 160.2 %shard_map.73 = f32[16384,128]{1,0:T(8,128)} custom-call(bf16[8,128,2048]{2,1,0:T(8,128)(2,1)} %bitcast.4, bf16[1,2048,2048]{2,1,0:T(8,128)(2,1)} %factor_hbm.1, bf16[1,2048,1024]{2,1,0:T(8,128)(2,1)} %right_hbm.1, s32[128,1024]{1,0:T(8,128)} %iface_hbm.1, f32[1,2048]{1,0:T(1,128)} %bitcast.5, f32[2,2048]{1,0:T(2,128)} %rows_hbm.1, f32[2,1024]{1,0:T(2,128)} %cols_hbm.1), custom_call_target="tpu_custom_call" | custom-call | tf_op jit(solution)/shard_map/pallas_call | solution.py:437
  160.2 6.6 %shard_map.74 = f32[2048,1024]{1,0:T(8,128)} custom-call(f32[32,512,128]{2,1,0:T(8,128)} %bitcast.3), custom_call_target="tpu_custom_call" | custom-call | tf_op jit(solution)/shard_map/pallas_call | solution.py:477

commit v3 on v2

--- a/solution.py
+++ b/solution.py
@@ -340,7 +340,7 @@
         pltpu.make_async_copy(src, dst, recv_sem2.at[order]).start()
 
         def one_back(o, carry):
-            o = (o * 11) % 32
+            o = (o * 7) % 32
             px, py, pzb = (x + o % 4) % 4, (y + o // 4 % 4) % 4, (zb + o // 16) % 2
             src, dst = back(px, py, pzb)
             pltpu.make_async_remote_copy(

time: 168 us -> 164 us (0.976)
  Pallas kernels: 167 us -> 164 us
    pallas_call x1, Pallas kernels: 160 us -> 157 us  [body(): pl.pallas_call(kernel, out_shape=jax.ShapeDtypeStruct((STRIPS * TILE_PITC...]
where the time goes in v3:
time: 164 us
  Pallas kernels  164 us (100%)
    pallas_call x1, Pallas kernels, body(): pl.pallas_call(kernel, out_shape=jax.ShapeDtypeStruct((STRIPS * TILE_PITC...  157 us
    pallas_call x1, Pallas kernels, body(): pl.pallas_call(merge, out_shape=jax.ShapeDtypeStruct((2048, 1024), F32),...  6.62 us

profile of v3, /device:TPU:1, one launch (start us, length us, event | category | flops | bytes accessed | tf_op | source)
XLA Modules:
  0.0 163.8 jit_solution(4223175282828823673)
XLA Ops:
  0.0 157.2 %shard_map.73 = f32[16384,128]{1,0:T(8,128)} custom-call(bf16[8,128,2048]{2,1,0:T(8,128)(2,1)} %bitcast.4, bf16[1,2048,2048]{2,1,0:T(8,128)(2,1)} %factor_hbm.1, bf16[1,2048,1024]{2,1,0:T(8,128)(2,1)} %right_hbm.1, s32[128,1024]{1,0:T(8,128)} %iface_hbm.1, f32[1,2048]{1,0:T(1,128)} %bitcast.5, f32[2,2048]{1,0:T(2,128)} %rows_hbm.1, f32[2,1024]{1,0:T(2,128)} %cols_hbm.1), custom_call_target="tpu_custom_call" | custom-call | tf_op jit(solution)/shard_map/pallas_call | solution.py:437
  157.2 6.6 %shard_map.74 = f32[2048,1024]{1,0:T(8,128)} custom-call(f32[32,512,128]{2,1,0:T(8,128)} %bitcast.3), custom_call_target="tpu_custom_call" | custom-call | tf_op jit(solution)/shard_map/pallas_call | solution.py:477
